TPU v7x, 128 devices: a whole 4x4x4 slice. The times are simulated.
128 devices in a mesh: row: 16 (over x, z), col: 8 (over y, core).
Axes of the slice: x: 4, y: 4, z: 4, core: 2. Of those that a mesh axis runs over, the one named last changes fastest.
Arguments:
- front: float32 [9216, 9216], P('row', 'col')
- child_tiles: float32 [16384, 4096], P(('row', 'col')), may hold values from -0.4375 to 0.4375
- tile_target: int32 [16384], P(('row', 'col')), may hold values from 0 to 20735, as said below
- tile_count: int32 [512], P(('row', 'col')), may hold values from 24 to 32
- probe: float32 [9216, 512], P('col'), may hold values from -1.75 to 1.75
Outputs:
- panel_factor: float32 [9216, 1024], P('row', 'col')
- sketch: float32 [9216, 512], P('row', 'col')
Inputs may be any that keep to these rules, and one draw needn't show every extreme that they name: `tile_target`: among the 128 slots of one device, live or not, each counted once at its target tile and once at the mirrored tile, at most 2 placements fall inside the block of the front held by any one device.
All inputs are finite; a program needn't handle non-finite values.
Results may differ from a plain program's by a relative error of at most 0.00015.
Values sent between devices are 32-bit elements; how exact they have to be, the bound alone decides.
A program may use at most 128 MiB of HBM per device.

v0:
```python
import jax
import jax.numpy as jnp
from jax import lax
from jax.sharding import PartitionSpec as P

NB = 512
PANELS = 2
TB = 64
SLOTS = 32
HIGH = lax.Precision.HIGHEST


def in_blocks(value, dim, size):
    before, after = (value.shape[:dim], value.shape[dim + 1 :])
    return jnp.moveaxis(value.reshape(*before, size, -1, *after), dim, 0)


def joined_along(tiles, dim):
    lengths = list(tiles.shape[1:])
    lengths[dim] *= tiles.shape[0]
    return jnp.moveaxis(tiles, 0, dim).reshape(lengths)


def one_exchange(value, axis, axes, splits, concats):
    sizes = [lax.axis_size(a) for a in axes]
    tiles = in_blocks(value, splits[0], sizes[0])
    tiles = jnp.moveaxis(in_blocks(tiles, splits[1] + 1, sizes[1]), 0, 1)
    inside = tiles.shape[2:]
    tiles = tiles.reshape(-1, *inside)
    tiles = lax.all_to_all(tiles, axis, split_axis=0, concat_axis=0, tiled=True)
    tiles = joined_along(tiles.reshape(*sizes, *inside), concats[0] + 1)
    return joined_along(tiles, concats[1])


def filled_up(lines, size):
    spare = -lines.shape[0] % size
    if not spare:
        return lines
    return jnp.concatenate([lines, jnp.zeros((spare, *lines.shape[1:]), lines.dtype)])


def from_root(value, axis, root):
    lines = jnp.where(lax.axis_index(axis) == root, value, jnp.zeros_like(value)).reshape(
        -1, *value.shape[1:][-1:]
    )
    padded = filled_up(lines, lax.axis_size(axis))
    own = lax.psum_scatter(padded, axis, scatter_dimension=0, tiled=True)
    return lax.all_gather(own, axis, axis=0, tiled=True)[: len(lines)].reshape(value.shape)


def broadcast(value, axis, root):
    mine = lax.axis_index(axis) == root
    return lax.psum(jnp.where(mine, value, jnp.zeros_like(value)), axis)


def sum_at_owner(value, axis, dim):
    tiles = in_blocks(value, dim, lax.axis_size(axis))
    arrived = lax.all_to_all(tiles, axis, split_axis=0, concat_axis=0, tiled=True)
    return arrived.sum(axis=0)


def per_device(front, child_tiles, tile_target, tile_count, probe):
    row_count = lax.axis_size("row")
    col_count = lax.axis_size("col")
    devices = row_count * col_count
    local_rows, local_cols = front.shape
    tile_rows = local_rows // TB
    tile_cols = local_cols // TB
    grid = tile_cols * col_count
    local_tiles = tile_rows * tile_cols
    held = child_tiles.shape[0]
    capacity = 2 * max(1, (held + devices - 1) // devices)
    slot_index = jnp.arange(held, dtype=jnp.int32)
    live_once = slot_index % SLOTS < tile_count[slot_index // SLOTS]
    live = jnp.concatenate([live_once, live_once])
    mirrored = child_tiles.reshape(held, TB, TB).transpose(0, 2, 1).reshape(held, TB * TB)
    placements = jnp.concatenate([child_tiles, mirrored], axis=0)
    first_row = tile_target // grid
    first_col = tile_target % grid
    target_row = jnp.concatenate([first_row, first_col])
    target_col = jnp.concatenate([first_col, first_row])
    owner = target_row // tile_rows * col_count + target_col // tile_cols
    place = target_row % tile_rows * tile_cols + target_col % tile_cols
    onehot = (
        (owner[:, None] == jnp.arange(devices, dtype=jnp.int32)[None, :]) & live[:, None]
    ).astype(jnp.int32)
    earlier = jnp.cumsum(onehot, axis=0) - onehot
    rank = jnp.sum(earlier * onehot, axis=1)
    slot = jnp.where(live, owner * capacity + rank, devices * capacity)
    outgoing = (
        jnp.zeros((devices * capacity + 1, TB * TB), jnp.float32).at[slot].set(placements)[:-1]
    )
    where_to = jnp.full((devices * capacity + 1,), local_tiles, jnp.int32).at[slot].set(place)[:-1]
    shaped = (
        outgoing.reshape(row_count, col_count * capacity, TB * TB),
        where_to.reshape(row_count, col_count * capacity),
    )
    incoming, landing = (
        one_exchange(shaped[0], ("row", "col"), ("row", "col"), (0, 1), (0, 1)),
        one_exchange(shaped[1], ("row", "col"), ("row", "col"), (0, 1), (0, 1)),
    )
    incoming = incoming.reshape(-1, TB * TB)
    landing = landing.reshape(-1)
    extend = (
        jnp.zeros((local_tiles + 1, TB * TB), jnp.float32).at[landing].add(incoming)[:local_tiles]
    )
    extend = (
        extend.reshape(tile_rows, tile_cols, TB, TB)
        .transpose(0, 2, 1, 3)
        .reshape(local_rows, local_cols)
    )
    matrix = front + extend
    row_start = lax.axis_index("row") * local_rows
    col_start = lax.axis_index("col") * local_cols
    global_rows = row_start + jnp.arange(local_rows, dtype=jnp.int32)
    group = row_count // col_count
    margin = jnp.zeros((NB, NB), jnp.float32)
    factor_parts = []
    for k in range(PANELS):
        low = k * NB
        high = low + NB
        owner_col = low // local_cols
        offset = low % local_cols
        panel = from_root(matrix[:, offset : offset + NB], "col", owner_col)
        padded = jnp.concatenate([margin, panel, margin], axis=0)
        begin = jnp.clip(low - row_start + NB, 0, local_rows + NB)
        piece = lax.dynamic_slice_in_dim(padded, begin, NB, 0)
        diag_block = lax.psum(piece, "row")
        chol = jnp.linalg.cholesky(0.5 * (diag_block + diag_block.T))
        solved = jax.scipy.linalg.solve_triangular(chol, panel.T, lower=True).T
        factor_parts.append(jnp.where((global_rows >= low)[:, None], solved, 0.0))
        trail = jnp.where((global_rows >= high)[:, None], solved, 0.0)
        column_owner = lax.axis_index("col") * group
        pieces = [broadcast(trail, "row", column_owner + member) for member in range(group)]
        across = jnp.concatenate(pieces, axis=0)
        matrix = matrix - jnp.dot(trail, across.T, precision=HIGH)
    start = PANELS * NB
    global_cols = col_start + jnp.arange(local_cols, dtype=jnp.int32)
    weighted = jnp.where((global_cols >= start)[:, None], probe, 0.0)
    shares = sum_at_owner(
        lax.dot_general(weighted, matrix, (((0,), (1,)), ((), ())), precision=HIGH), "col", 0
    )
    sketch = jnp.where((global_rows >= start)[:, None], shares.T, 0.0)
    all_panels = jnp.concatenate(factor_parts, axis=1)
    width = all_panels.shape[1] // col_count
    panel_factor = lax.dynamic_slice_in_dim(all_panels, lax.axis_index("col") * width, width, 1)
    return (panel_factor, sketch)


def solution(mesh):
    return jax.shard_map(
        per_device,
        mesh=mesh,
        in_specs=(
            P("row", "col"),
            P(("row", "col"), None),
            P(("row", "col")),
            P(("row", "col")),
            P("col", None),
        ),
        out_specs=(P("row", "col"), P("row", "col")),
        check_vma=False,
    )
```

profile of v0, /device:TPU:1, one launch (start us, length us, event | category | flops | bytes accessed | tf_op | source)
XLA Modules:
  0.0 1003.4 jit_solution(17757820655012956910)
XLA Ops:
  17.6 11.5 %all-to-all-start = ((s32[128,1,2]{2,1,0:T(1,128)}), s32[128,1,2]{2,1,0:T(1,128)S(1)}, u32[]{:S(2)}, u32[]{:S(2)}) async-start(s32[128,1,2]{2,1,0:T(1,128)} %bitcast.16), calls=%async_computation | async-start | bytes 131072 | tf_op jit(solution)/shard_map/all_to_all | solution.py:30
  57.4 10.2 %all-to-all-start.1 = ((f32[128,1,2,4096]{3,2,1,0:T(2,128)}), f32[128,1,2,4096]{3,2,1,0:T(2,128)}, u32[]{:S(2)}, u32[]{:S(2)}) async-start(f32[128,1,2,4096]{3,2,1,0:T(2,128)} %bitcast.188), calls=%async_computation.1 | async-start | bytes 8388608 | tf_op jit(solution)/shard_map/all_to_all | solution.py:30
  68.0 52.1 %all-to-all-done.1 = f32[128,1,2,4096]{3,2,1,0:T(2,128)} async-done(((f32[128,1,2,4096]{3,2,1,0:T(2,128)}), f32[128,1,2,4096]{3,2,1,0:T(2,128)}, u32[]{:S(2)}, u32[]{:S(2)}) %all-to-all-start.1) | async-done | bytes 4194336 | tf_op jit(solution)/shard_map/all_to_all | solution.py:30
  157.8 27.1 %reduce-scatter.3.cloned.1.call-done = f32[72,512]{1,0:T(8,128)} async-done(((f32[576,512]{1,0:T(8,128)}), f32[72,512]{1,0:T(8,128)}) %reduce-scatter.3.cloned.1.call-update) | async-done | bytes 147472 | tf_op jit(solution)/shard_map/reduce_scatter | solution.py:47
  184.9 27.1 %all-gather.3.cloned.1.call-done = f32[576,512]{1,0:T(8,128)} async-done(((f32[72,512]{1,0:T(8,128)}), f32[576,512]{1,0:T(8,128)}) %all-gather.3.cloned.1.call-update) | async-done | bytes 1179664 | tf_op jit(solution)/shard_map/all_gather | solution.py:48
  216.5 84.9 %all-reduce.8.cloned.1.call-done = f32[512,512]{1,0:T(8,128)} async-done(((f32[512,512]{1,0:T(8,128)}), f32[512,512]{1,0:T(8,128)}) %all-reduce.8.cloned.1.call-update) | async-done | bytes 1048592 | tf_op jit(solution)/shard_map/psum | solution.py:128
  312.1 11.7 %cholesky.286 = f32[128,128]{1,0:T(8,128)S(1)} custom-call(f32[128,128]{1,0:T(8,128)S(1)} %cholesky.426), custom_call_target="Cholesky" | custom-call | tf_op jit(solution)/shard_map/jit(cholesky)/cholesky | solution.py:129
  338.0 11.7 %cholesky.305 = f32[128,128]{1,0:T(8,128)S(1)} custom-call(f32[128,128]{1,0:T(8,128)S(1)} %cholesky.430), custom_call_target="Cholesky" | custom-call | tf_op jit(solution)/shard_map/jit(cholesky)/cholesky | solution.py:129
  362.7 11.7 %cholesky.326 = f32[128,128]{1,0:T(8,128)S(1)} custom-call(f32[128,128]{1,0:T(8,128)S(1)} %cholesky.435), custom_call_target="Cholesky" | custom-call | tf_op jit(solution)/shard_map/jit(cholesky)/cholesky | solution.py:129
  387.8 12.1 %cholesky.343 = f32[128,128]{1,0:T(8,128)S(1)} custom-call(f32[128,128]{1,0:T(8,128)S(1)} %convolution_subtract_fusion.13), custom_call_target="Cholesky" | custom-call | tf_op jit(solution)/shard_map/jit(cholesky)/cholesky | solution.py:129
  406.8 11.9 %while.4 = (s32[]{:T(128)}, f32[512,512]{1,0:T(8,128)}, s32[4,2]{0,1:T(2,128)S(1)}, f32[4,128,128]{2,1,0:T(8,128)S(1)}, s32[]{:T(128)}) while((s32[]{:T(128)}, f32[512,512]{1,0:T(8,128)}, s32[4,2]{0,1:T(2,128)S(1)}, f32[4,128,128]{2,1,0:T(8,128)S(1)}, s32[]{:T(128)}) %tuple.68), condition=%wide.while_cond, body=%wide.while_body.sunk | while | flops 2 | bytes 131181 | solution.py:130
  418.8 39.3 %custom-call.30 = f32[4,128,128]{1,2,0:T(8,128)S(1)} custom-call(f32[4,128,128]{2,1,0:T(8,128)S(1)} %get-tuple-element.18), custom_call_target="InvertDiagBlocksLowerTriangular" | custom-call | tf_op jit(solution)/shard_map/jit(_solve_triangular)/triangular_solve | solution.py:130
  469.5 91.7 %all-reduce.14.cloned.1.call-done = (f32[576,512]{1,0:T(8,128)}, f32[576,512]{1,0:T(8,128)}) async-done(((f32[576,512]{1,0:T(8,128)}, f32[576,512]{1,0:T(8,128)}), (f32[576,512]{1,0:T(8,128)}, f32[576,512]{1,0:T(8,128)})) %all-reduce.14.cloned.1.call-update) | async-done | bytes 2359312 | tf_op jit(solution)/shard_map/psum | solution.py:53
  570.8 30.4 %reduce-scatter.5.cloned.1.call-done = f32[72,512]{1,0:T(8,128)} async-done(((f32[576,512]{1,0:T(8,128)}), f32[72,512]{1,0:T(8,128)}) %reduce-scatter.5.cloned.1.call-update) | async-done | bytes 147472 | tf_op jit(solution)/shard_map/reduce_scatter | solution.py:47
  601.3 26.9 %all-gather.5.cloned.1.call-done = f32[576,512]{1,0:T(8,128)} async-done(((f32[72,512]{1,0:T(8,128)}), f32[576,512]{1,0:T(8,128)}) %all-gather.5.cloned.1.call-update) | async-done | bytes 1179664 | tf_op jit(solution)/shard_map/all_gather | solution.py:48
  631.0 86.2 %all-reduce.10.cloned.1.call-done = f32[512,512]{1,0:T(8,128)} async-done(((f32[512,512]{1,0:T(8,128)}), f32[512,512]{1,0:T(8,128)}) %all-reduce.10.cloned.1.call-update) | async-done | bytes 1048592 | tf_op jit(solution)/shard_map/psum | solution.py:128
  720.1 11.7 %cholesky.358 = f32[128,128]{1,0:T(8,128)S(1)} custom-call(f32[128,128]{1,0:T(8,128)S(1)} %cholesky.439), custom_call_target="Cholesky" | custom-call | tf_op jit(solution)/shard_map/jit(cholesky)/cholesky | solution.py:129
  742.5 11.7 %cholesky.377 = f32[128,128]{1,0:T(8,128)S(1)} custom-call(f32[128,128]{1,0:T(8,128)S(1)} %cholesky.443), custom_call_target="Cholesky" | custom-call | tf_op jit(solution)/shard_map/jit(cholesky)/cholesky | solution.py:129
  766.4 11.7 %cholesky.398 = f32[128,128]{1,0:T(8,128)S(1)} custom-call(f32[128,128]{1,0:T(8,128)S(1)} %cholesky.448), custom_call_target="Cholesky" | custom-call | tf_op jit(solution)/shard_map/jit(cholesky)/cholesky | solution.py:129
  789.2 11.9 %cholesky.415 = f32[128,128]{1,0:T(8,128)S(1)} custom-call(f32[128,128]{1,0:T(8,128)S(1)} %convolution_subtract_fusion.12), custom_call_target="Cholesky" | custom-call | tf_op jit(solution)/shard_map/jit(cholesky)/cholesky | solution.py:129
  812.1 39.3 %custom-call.34 = f32[4,128,128]{1,2,0:T(8,128)S(1)} custom-call(f32[4,128,128]{2,1,0:T(8,128)S(1)} %get-tuple-element.19), custom_call_target="InvertDiagBlocksLowerTriangular" | custom-call | tf_op jit(solution)/shard_map/jit(_solve_triangular)/triangular_solve | solution.py:130
  859.8 91.7 %all-reduce.12.cloned.1.call-done = (f32[576,512]{1,0:T(8,128)}, f32[576,512]{1,0:T(8,128)}) async-done(((f32[576,512]{1,0:T(8,128)}, f32[576,512]{1,0:T(8,128)}), (f32[576,512]{1,0:T(8,128)}, f32[576,512]{1,0:T(8,128)})) %all-reduce.12.cloned.1.call-update) | async-done | bytes 2359312 | tf_op jit(solution)/shard_map/psum | solution.py:53
  958.6 12.7 %fusion.6 = f32[512,576]{1,0:T(8,128)} fusion(f32[576,1152]{1,0:T(8,128)S(1)} %convolution_subtract_fusion, f32[1152,512]{1,0:T(8,128)S(1)} %copy-done.12, pred[1152]{0:T(1024)(128)(4,1)S(1)} %add_compare_fusion), kind=kOutput, calls=%fused_computation.24 | convolution fusion | flops 4077453312 | bytes 6194304 | tf_op jit(solution)/shard_map/dot_general | solution.py:141
  978.6 17.0 %all-to-all-done.2 = f32[8,64,576]{2,1,0:T(8,128)S(1)} async-done(((f32[8,64,576]{2,1,0:T(8,128)}), f32[8,64,576]{2,1,0:T(8,128)S(1)}, u32[]{:S(2)}, u32[]{:S(2)}) %all-to-all-start.2) | async-done | bytes 1179680 | tf_op jit(solution)/shard_map/all_to_all | solution.py:58
  (195 shorter events, 248.6 us)
Async XLA Ops:
  17.6 39.7 %all-to-all-start = ((s32[128,1,2]{2,1,0:T(1,128)}), s32[128,1,2]{2,1,0:T(1,128)S(1)}, u32[]{:S(2)}, u32[]{:S(2)}) async-start(s32[128,1,2]{2,1,0:T(1,128)} %bitcast.16), calls=%async_computation | async-start | bytes 131072 | tf_op jit(solution)/shard_map/all_to_all | solution.py:30
  57.4 62.7 %all-to-all-start.1 = ((f32[128,1,2,4096]{3,2,1,0:T(2,128)}), f32[128,1,2,4096]{3,2,1,0:T(2,128)}, u32[]{:S(2)}, u32[]{:S(2)}) async-start(f32[128,1,2,4096]{3,2,1,0:T(2,128)} %bitcast.188), calls=%async_computation.1 | async-start | bytes 8388608 | tf_op jit(solution)/shard_map/all_to_all | solution.py:30
  67.6 117.3 %reduce-scatter.3.cloned.1.call-start = ((), (), s32[]{:S(2)}) async-start(), calls=%async_computation.5 | async-start | bytes 1327104 | tf_op jit(solution)/shard_map/reduce_scatter | solution.py:47
  157.7 54.3 %all-gather.3.cloned.1.call-start = ((), (), s32[]{:S(2)}) async-start(), calls=%async_computation.6 | async-start | bytes 1327104 | tf_op jit(solution)/shard_map/all_gather | solution.py:48
  184.9 116.6 %all-reduce.8.cloned.1.call-start = ((), (), s32[]{:S(2)}) async-start(), calls=%async_computation.7 | async-start | bytes 2097152 | tf_op jit(solution)/shard_map/psum | solution.py:128
  216.0 345.1 %all-reduce.14.cloned.1.call-start = ((), (), s32[]{:S(2)}) async-start(), calls=%async_computation.12 | async-start | bytes 4718592 | tf_op jit(solution)/shard_map/psum | solution.py:53
  311.1 1.0 copy-start.9
  458.1 3.3 copy-start.13
  458.1 3.3 copy-start.4
  467.3 2.1 copy-start.11
  469.4 131.8 %reduce-scatter.5.cloned.1.call-start = ((), (), s32[]{:S(2)}) async-start(), calls=%async_computation.8 | async-start | bytes 1327104 | tf_op jit(solution)/shard_map/reduce_scatter | solution.py:47
  568.0 1.5 copy-start
  570.7 57.5 %copy-start.3 = (f32[512,512]{1,0:T(8,128)S(1)}, f32[512,512]{1,0:T(8,128)}, u32[]{:S(2)}) copy-start(f32[512,512]{1,0:T(8,128)} %copy-done.2) | copy-start | bytes 3145732
  570.8 57.4 %all-gather.5.cloned.1.call-start = ((), (), s32[]{:S(2)}) async-start(), calls=%async_computation.9 | async-start | bytes 1327104 | tf_op jit(solution)/shard_map/all_gather | solution.py:48
  601.3 116.0 %all-reduce.10.cloned.1.call-start = ((), (), s32[]{:S(2)}) async-start(), calls=%async_computation.10 | async-start | bytes 2097152 | tf_op jit(solution)/shard_map/psum | solution.py:128
  630.8 320.8 %all-reduce.12.cloned.1.call-start = ((), (), s32[]{:S(2)}) async-start(), calls=%async_computation.11 | async-start | bytes 4718592 | tf_op jit(solution)/shard_map/psum | solution.py:53
  717.2 1.7 copy-start.7
  804.3 47.2 %copy-start.5 = (f32[576,512]{1,0:T(8,128)S(1)}, f32[576,512]{1,0:T(8,128)}, u32[]{:S(2)}) copy-start(f32[576,512]{1,0:T(8,128)} %all-gather.5.cloned.1.call-done) | copy-start | bytes 3538948
  812.1 39.3 %copy-start.8 = (f32[512,512]{1,0:T(8,128)}, f32[512,512]{1,0:T(8,128)S(1)}, u32[]{:S(2)}) copy-start(f32[512,512]{1,0:T(8,128)S(1)} %get-tuple-element.216) | copy-start | bytes 3145732
  857.6 2.1 copy-start.10
  857.7 93.9 %copy-start.1 = (f32[576,1152]{1,0:T(8,128)S(1)}, f32[576,1152]{1,0:T(8,128)}, u32[]{:S(2)}) copy-start(f32[576,1152]{1,0:T(8,128)} %copy-done) | copy-start | bytes 7962628
  951.6 7.0 copy-start.12
  971.3 6.5 copy-start.6
  971.3 24.3 %all-to-all-start.2 = ((f32[8,64,576]{2,1,0:T(8,128)}), f32[8,64,576]{2,1,0:T(8,128)S(1)}, u32[]{:S(2)}, u32[]{:S(2)}) async-start(f32[8,64,576]{2,1,0:T(8,128)} %bitcast.63), calls=%async_computation.4 | async-start | bytes 2621440 | tf_op jit(solution)/shard_map/all_to_all | solution.py:58
  (1 other events, 1.0 us)
Sparse Core Ops, SparseCore 0:
  157.8 26.9 reduce-scatter.2
  186.5 25.4 all-gather.2
  216.2 85.2 all-reduce.7
  469.5 91.5 all-reduce.13
  570.9 30.2 reduce-scatter.4
  602.8 25.3 all-gather.4
  631.4 85.7 all-reduce.9
  859.9 91.6 all-reduce.11
where the time goes:
time: 1010 us; the launch traced here: 1000 us
  waiting for transfers between devices  535 us (53%)
  other arithmetic  280 us (28%)
  local copies, waits for them, and re-layouts  87.2 us (9%)
  matrix products  51.5 us (5%)
  starting transfers between devices  29.3 us (3%)
  between operations  20 us (2%)
    psum x2, waiting for transfers between devices, broadcast(): return lax.psum(jnp.where(mine, value, jnp.zeros_like(value)), axis)  183 us
    psum x2, waiting for transfers between devices, per_device(): diag_block = lax.psum(piece, 'row')  171 us
    another operation x29, other arithmetic, per_device(): chol = jnp.linalg.cholesky(0.5 * (diag_block + diag_block.T))  160 us
    another operation x5, other arithmetic, per_device(): solved = jax.scipy.linalg.solve_triangular(chol, panel.T, lower=True).T  81.2 us
    reduce_scatter x2, waiting for transfers between devices, from_root(): own = lax.psum_scatter(padded, axis, scatter_dimension=0, tiled=True)  57.5 us
    all_gather x2, waiting for transfers between devices, from_root(): lax.all_gather(own, axis, axis=0, tiled=True)[:len(lines)]  53.9 us
    all_to_all x2, waiting for transfers between devices, one_exchange(): tiles = lax.all_to_all(tiles, axis, split_axis=0, concat_axis=0, tiled=True)  52.1 us
    all_to_all x2, starting transfers between devices, one_exchange(): tiles = lax.all_to_all(tiles, axis, split_axis=0, concat_axis=0, tiled=True)  21.7 us
  transfers between devices with their start and end apart: 11, of which 10 were waited for; matrix products, arithmetic and copies ran while one was open for 3% of the time, Pallas kernels for 0%

commit v1 on v0

--- a/solution.py
+++ b/solution.py
@@ -125,7 +125,11 @@
         padded = jnp.concatenate([margin, panel, margin], axis=0)
         begin = jnp.clip(low - row_start + NB, 0, local_rows + NB)
         piece = lax.dynamic_slice_in_dim(padded, begin, NB, 0)
-        diag_block = lax.psum(piece, "row")
+        diag_block = piece
+        for hop in (1, 2, 4, 8):
+            diag_block = diag_block + lax.ppermute(
+                diag_block, "row", [(dev, dev ^ hop) for dev in range(16)]
+            )
         chol = jnp.linalg.cholesky(0.5 * (diag_block + diag_block.T))
         solved = jax.scipy.linalg.solve_triangular(chol, panel.T, lower=True).T
         factor_parts.append(jnp.where((global_rows >= low)[:, None], solved, 0.0))

time: 1010 us -> 1050 us (1.040)
  starting transfers between devices: 29.3 us -> 42.7 us
  waiting for transfers between devices: 535 us -> 547 us
    ppermute x0 -> x8, waiting for transfers between devices: none -> 179 us  [per_device(): lax.ppermute(diag_block, 'row', [(dev, dev ^ hop) for dev in range(16)])]
    psum x2 -> x0, waiting for transfers between devices: 171 us -> none  [per_device(): diag_block = lax.psum(piece, 'row')]
    ppermute x0 -> x8, starting transfers between devices: none -> 14 us  [per_device(): lax.ppermute(diag_block, 'row', [(dev, dev ^ hop) for dev in range(16)])]
  transfers between devices with their start and end apart: 11 -> 17, of which waited for: 10 -> 16; matrix products, arithmetic and copies ran while one was open for 3% -> 3% of each run, Pallas kernels for 0% -> 0%
where the time goes in v1:
time: 1050 us; the launch traced here: 1040 us
  waiting for transfers between devices  547 us (52%)
  other arithmetic  289 us (28%)
  local copies, waits for them, and re-layouts  88.9 us (8%)
  matrix products  50.2 us (5%)
  starting transfers between devices  42.7 us (4%)
  between operations  20.3 us (2%)
    psum x2, waiting for transfers between devices, broadcast(): return lax.psum(jnp.where(mine, value, jnp.zeros_like(value)), axis)  187 us
    ppermute x8, waiting for transfers between devices, per_device(): lax.ppermute(diag_block, 'row', [(dev, dev ^ hop) for dev in range(16)])  179 us
    another operation x29, other arithmetic, per_device(): chol = jnp.linalg.cholesky(0.5 * (diag_block + diag_block.T))  162 us
    another operation x5, other arithmetic, per_device(): solved = jax.scipy.linalg.solve_triangular(chol, panel.T, lower=True).T  81.1 us
    reduce_scatter x2, waiting for transfers between devices, from_root(): own = lax.psum_scatter(padded, axis, scatter_dimension=0, tiled=True)  57.5 us
    all_gather x2, waiting for transfers between devices, from_root(): lax.all_gather(own, axis, axis=0, tiled=True)[:len(lines)]  54 us
    all_to_all x2, waiting for transfers between devices, one_exchange(): tiles = lax.all_to_all(tiles, axis, split_axis=0, concat_axis=0, tiled=True)  52.1 us
    all_to_all x2, starting transfers between devices, one_exchange(): tiles = lax.all_to_all(tiles, axis, split_axis=0, concat_axis=0, tiled=True)  21.7 us
  transfers between devices with their start and end apart: 17, of which 16 were waited for; matrix products, arithmetic and copies ran while one was open for 3% of the time, Pallas kernels for 0%

profile of v1, /device:TPU:1, one launch (start us, length us, event | category | flops | bytes accessed | tf_op | source)
XLA Modules:
  0.0 1038.7 jit_solution(18342659583432440533)
XLA Ops:
  68.0 52.1 %all-to-all-done.1 = f32[128,1,2,4096]{3,2,1,0:T(2,128)} async-done(((f32[128,1,2,4096]{3,2,1,0:T(2,128)}), f32[128,1,2,4096]{3,2,1,0:T(2,128)}, u32[]{:S(2)}, u32[]{:S(2)}) %all-to-all-start.1) | async-done | bytes 4194336 | tf_op jit(solution)/shard_map/all_to_all | solution.py:30
  157.4 27.1 %reduce-scatter.3.cloned.1.call-done = f32[72,512]{1,0:T(8,128)} async-done(((f32[576,512]{1,0:T(8,128)}), f32[72,512]{1,0:T(8,128)}) %reduce-scatter.3.cloned.1.call-update) | async-done | bytes 147472 | tf_op jit(solution)/shard_map/reduce_scatter | solution.py:47
  184.5 27.1 %all-gather.3.cloned.1.call-done = f32[576,512]{1,0:T(8,128)} async-done(((f32[72,512]{1,0:T(8,128)}), f32[576,512]{1,0:T(8,128)}) %all-gather.3.cloned.1.call-update) | async-done | bytes 1179664 | tf_op jit(solution)/shard_map/all_gather | solution.py:48
  214.6 23.7 %collective-permute-done = f32[512,512]{1,0:T(8,128)S(1)} collective-permute-done((f32[512,512]{1,0:T(8,128)S(1)}, f32[512,512]{1,0:T(8,128)S(1)}, u32[]{:S(2)}, u32[]{:S(2)}) %collective-permute-start) | collective-permute-done | bytes 1048608 | tf_op jit(solution)/shard_map/ppermute | solution.py:130
  241.5 22.7 %collective-permute-done.1 = f32[512,512]{1,0:T(8,128)S(1)} collective-permute-done((f32[512,512]{1,0:T(8,128)S(1)}, f32[512,512]{1,0:T(8,128)S(1)}, u32[]{:S(2)}, u32[]{:S(2)}) %collective-permute-start.1) | collective-permute-done | bytes 1048608 | tf_op jit(solution)/shard_map/ppermute | solution.py:130
  265.2 22.0 %collective-permute-done.2 = f32[512,512]{1,0:T(8,128)S(1)} collective-permute-done((f32[512,512]{1,0:T(8,128)S(1)}, f32[512,512]{1,0:T(8,128)S(1)}, u32[]{:S(2)}, u32[]{:S(2)}) %collective-permute-start.2) | collective-permute-done | bytes 1048608 | tf_op jit(solution)/shard_map/ppermute | solution.py:130
  290.8 21.5 %collective-permute-done.3 = f32[512,512]{1,0:T(8,128)} collective-permute-done((f32[512,512]{1,0:T(8,128)}, f32[512,512]{1,0:T(8,128)}, u32[]{:S(2)}, u32[]{:S(2)}) %collective-permute-start.3) | collective-permute-done | bytes 1048608 | tf_op jit(solution)/shard_map/ppermute | solution.py:130
  325.7 11.7 %cholesky.286 = f32[128,128]{1,0:T(8,128)S(1)} custom-call(f32[128,128]{1,0:T(8,128)S(1)} %cholesky.426), custom_call_target="Cholesky" | custom-call | tf_op jit(solution)/shard_map/jit(cholesky)/cholesky | solution.py:133
  401.6 11.9 %cholesky.343 = f32[128,128]{1,0:T(8,128)S(1)} custom-call(f32[128,128]{1,0:T(8,128)S(1)} %convolution_subtract_fusion.13), custom_call_target="Cholesky" | custom-call | tf_op jit(solution)/shard_map/jit(cholesky)/cholesky | solution.py:133
  420.4 11.8 %while.4 = (s32[]{:T(128)}, f32[512,512]{1,0:T(8,128)}, s32[4,2]{0,1:T(2,128)S(1)}, f32[4,128,128]{2,1,0:T(8,128)S(1)}, s32[]{:T(128)}) while((s32[]{:T(128)}, f32[512,512]{1,0:T(8,128)}, s32[4,2]{0,1:T(2,128)S(1)}, f32[4,128,128]{2,1,0:T(8,128)S(1)}, s32[]{:T(128)}) %tuple.68), condition=%wide.while_cond, body=%wide.while_body.sunk | while | flops 2 | bytes 131181 | solution.py:134
  432.2 39.3 %custom-call.30 = f32[4,128,128]{1,2,0:T(8,128)S(1)} custom-call(f32[4,128,128]{2,1,0:T(8,128)S(1)} %get-tuple-element.18), custom_call_target="InvertDiagBlocksLowerTriangular" | custom-call | tf_op jit(solution)/shard_map/jit(_solve_triangular)/triangular_solve | solution.py:134
  479.9 93.7 %all-reduce.8.cloned.1.call-done = (f32[576,512]{1,0:T(8,128)}, f32[576,512]{1,0:T(8,128)}) async-done(((f32[576,512]{1,0:T(8,128)}, f32[576,512]{1,0:T(8,128)}), (f32[576,512]{1,0:T(8,128)}, f32[576,512]{1,0:T(8,128)})) %all-reduce.8.cloned.1.call-update) | async-done | bytes 2359312 | tf_op jit(solution)/shard_map/psum | solution.py:53
  584.0 30.4 %reduce-scatter.5.cloned.1.call-done = f32[72,512]{1,0:T(8,128)} async-done(((f32[576,512]{1,0:T(8,128)}), f32[72,512]{1,0:T(8,128)}) %reduce-scatter.5.cloned.1.call-update) | async-done | bytes 147472 | tf_op jit(solution)/shard_map/reduce_scatter | solution.py:47
  614.4 26.9 %all-gather.5.cloned.1.call-done = f32[576,512]{1,0:T(8,128)} async-done(((f32[72,512]{1,0:T(8,128)}), f32[576,512]{1,0:T(8,128)}) %all-gather.5.cloned.1.call-update) | async-done | bytes 1179664 | tf_op jit(solution)/shard_map/all_gather | solution.py:48
  644.7 23.1 %collective-permute-done.4 = f32[512,512]{1,0:T(8,128)S(1)} collective-permute-done((f32[512,512]{1,0:T(8,128)S(1)}, f32[512,512]{1,0:T(8,128)S(1)}, u32[]{:S(2)}, u32[]{:S(2)}) %collective-permute-start.4) | collective-permute-done | bytes 1048608 | tf_op jit(solution)/shard_map/ppermute | solution.py:130
  671.2 22.7 %collective-permute-done.5 = f32[512,512]{1,0:T(8,128)S(1)} collective-permute-done((f32[512,512]{1,0:T(8,128)S(1)}, f32[512,512]{1,0:T(8,128)S(1)}, u32[]{:S(2)}, u32[]{:S(2)}) %collective-permute-start.5) | collective-permute-done | bytes 1048608 | tf_op jit(solution)/shard_map/ppermute | solution.py:130
  694.8 22.1 %collective-permute-done.6 = f32[512,512]{1,0:T(8,128)S(1)} collective-permute-done((f32[512,512]{1,0:T(8,128)S(1)}, f32[512,512]{1,0:T(8,128)S(1)}, u32[]{:S(2)}, u32[]{:S(2)}) %collective-permute-start.6) | collective-permute-done | bytes 1048608 | tf_op jit(solution)/shard_map/ppermute | solution.py:130
  719.8 21.4 %collective-permute-done.7 = f32[512,512]{1,0:T(8,128)} collective-permute-done((f32[512,512]{1,0:T(8,128)S(1)}, f32[512,512]{1,0:T(8,128)}, u32[]{:S(2)}, u32[]{:S(2)}) %collective-permute-start.7) | collective-permute-done | bytes 1048608 | tf_op jit(solution)/shard_map/ppermute | solution.py:130
  772.1 12.3 %cholesky.377 = f32[128,128]{1,0:T(8,128)} custom-call(f32[128,128]{1,0:T(8,128)S(1)} %cholesky.443), custom_call_target="Cholesky" | custom-call | tf_op jit(solution)/shard_map/jit(cholesky)/cholesky | solution.py:133
  821.5 11.9 %cholesky.415 = f32[128,128]{1,0:T(8,128)S(1)} custom-call(f32[128,128]{1,0:T(8,128)S(1)} %convolution_subtract_fusion.12), custom_call_target="Cholesky" | custom-call | tf_op jit(solution)/shard_map/jit(cholesky)/cholesky | solution.py:133
  845.4 39.3 %custom-call.34 = f32[4,128,128]{1,2,0:T(8,128)S(1)} custom-call(f32[4,128,128]{2,1,0:T(8,128)S(1)} %get-tuple-element.19), custom_call_target="InvertDiagBlocksLowerTriangular" | custom-call | tf_op jit(solution)/shard_map/jit(_solve_triangular)/triangular_solve | solution.py:134
  893.1 93.5 %all-reduce.6.cloned.1.call-done = (f32[576,512]{1,0:T(8,128)}, f32[576,512]{1,0:T(8,128)}) async-done(((f32[576,512]{1,0:T(8,128)}, f32[576,512]{1,0:T(8,128)}), (f32[576,512]{1,0:T(8,128)}, f32[576,512]{1,0:T(8,128)})) %all-reduce.6.cloned.1.call-update) | async-done | bytes 2359312 | tf_op jit(solution)/shard_map/psum | solution.py:53
  993.6 12.7 %fusion.6 = f32[512,576]{1,0:T(8,128)} fusion(f32[576,1152]{1,0:T(8,128)S(1)} %convolution_subtract_fusion, f32[1152,512]{1,0:T(8,128)S(1)} %copy-done.11, pred[1152]{0:T(1024)(128)(4,1)S(1)} %add_compare_fusion), kind=kOutput, calls=%fused_computation.24 | convolution fusion | flops 4077453312 | bytes 6194304 | tf_op jit(solution)/shard_map/dot_general | solution.py:145
  1013.6 17.0 %all-to-all-done.2 = f32[8,64,576]{2,1,0:T(8,128)S(1)} async-done(((f32[8,64,576]{2,1,0:T(8,128)}), f32[8,64,576]{2,1,0:T(8,128)S(1)}, u32[]{:S(2)}, u32[]{:S(2)}) %all-to-all-start.2) | async-done | bytes 1179680 | tf_op jit(solution)/shard_map/all_to_all | solution.py:58
  (209 shorter events, 340.6 us)
Async XLA Ops:
  17.6 39.7 %all-to-all-start = ((s32[128,1,2]{2,1,0:T(1,128)}), s32[128,1,2]{2,1,0:T(1,128)S(1)}, u32[]{:S(2)}, u32[]{:S(2)}) async-start(s32[128,1,2]{2,1,0:T(1,128)} %bitcast.16), calls=%async_computation | async-start | bytes 131072 | tf_op jit(solution)/shard_map/all_to_all | solution.py:30
  57.4 62.7 %all-to-all-start.1 = ((f32[128,1,2,4096]{3,2,1,0:T(2,128)}), f32[128,1,2,4096]{3,2,1,0:T(2,128)}, u32[]{:S(2)}, u32[]{:S(2)}) async-start(f32[128,1,2,4096]{3,2,1,0:T(2,128)} %bitcast.188), calls=%async_computation.1 | async-start | bytes 8388608 | tf_op jit(solution)/shard_map/all_to_all | solution.py:30
  67.6 116.9 %reduce-scatter.3.cloned.1.call-start = ((), (), s32[]{:S(2)}) async-start(), calls=%async_computation.5 | async-start | bytes 1327104 | tf_op jit(solution)/shard_map/reduce_scatter | solution.py:47
  157.3 54.3 %all-gather.3.cloned.1.call-start = ((), (), s32[]{:S(2)}) async-start(), calls=%async_computation.6 | async-start | bytes 1327104 | tf_op jit(solution)/shard_map/all_gather | solution.py:48
  184.5 389.1 %all-reduce.8.cloned.1.call-start = ((), (), s32[]{:S(2)}) async-start(), calls=%async_computation.10 | async-start | bytes 4718592 | tf_op jit(solution)/shard_map/psum | solution.py:53
  211.7 26.6 %copy-start.3 = (f32[576,512]{1,0:T(8,128)S(1)}, f32[576,512]{1,0:T(8,128)}, u32[]{:S(2)}) copy-start(f32[576,512]{1,0:T(8,128)} %all-gather.3.cloned.1.call-done) | copy-start | bytes 3538948
  213.8 24.5 %collective-permute-start = (f32[512,512]{1,0:T(8,128)S(1)}, f32[512,512]{1,0:T(8,128)S(1)}, u32[]{:S(2)}, u32[]{:S(2)}) collective-permute-start(f32[512,512]{1,0:T(8,128)S(1)} %fusion.17), channel_id=1, source_target_pairs={{0,8},{8,0},{16,24},{24,16},{32,40},{40,32},{48,56},{56,48},{64,72... | collective-permute-start | bytes 3145736 | tf_op jit(solution)/shard_map/ppermute | solution.py:130
  239.1 25.2 %collective-permute-start.1 = (f32[512,512]{1,0:T(8,128)S(1)}, f32[512,512]{1,0:T(8,128)S(1)}, u32[]{:S(2)}, u32[]{:S(2)}) collective-permute-start(f32[512,512]{1,0:T(8,128)S(1)} %fusion.130), channel_id=1, source_target_pairs={{0,16},{8,24},{16,0},{24,8},{32,48},{40,56},{48,32},{56,40},{64,80... | collective-permute-start | bytes 3145736 | tf_op jit(solution)/shard_map/ppermute | solution.py:130
  264.5 22.8 %collective-permute-start.2 = (f32[512,512]{1,0:T(8,128)S(1)}, f32[512,512]{1,0:T(8,128)S(1)}, u32[]{:S(2)}, u32[]{:S(2)}) collective-permute-start(f32[512,512]{1,0:T(8,128)S(1)} %add.271), channel_id=1, source_target_pairs={{0,32},{8,40},{16,48},{24,56},{32,0},{40,8},{48,16},{56,24},{64,96... | collective-permute-start | bytes 3145736 | tf_op jit(solution)/shard_map/ppermute | solution.py:130
  288.5 23.8 %collective-permute-start.3 = (f32[512,512]{1,0:T(8,128)}, f32[512,512]{1,0:T(8,128)}, u32[]{:S(2)}, u32[]{:S(2)}) collective-permute-start(f32[512,512]{1,0:T(8,128)} %add.272), channel_id=1, source_target_pairs={{0,64},{8,72},{16,80},{24,88},{32,96},{40,104},{48,112},{56,120},{... | collective-permute-start | bytes 3145736 | tf_op jit(solution)/shard_map/ppermute | solution.py:130
  479.9 134.5 %reduce-scatter.5.cloned.1.call-start = ((), (), s32[]{:S(2)}) async-start(), calls=%async_computation.7 | async-start | bytes 1327104 | tf_op jit(solution)/shard_map/reduce_scatter | solution.py:47
  583.9 57.4 %all-gather.5.cloned.1.call-start = ((), (), s32[]{:S(2)}) async-start(), calls=%async_computation.8 | async-start | bytes 1327104 | tf_op jit(solution)/shard_map/all_gather | solution.py:48
  614.4 372.2 %all-reduce.6.cloned.1.call-start = ((), (), s32[]{:S(2)}) async-start(), calls=%async_computation.9 | async-start | bytes 4718592 | tf_op jit(solution)/shard_map/psum | solution.py:53
  641.4 26.4 %copy-start.4 = (f32[576,512]{1,0:T(8,128)S(1)}, f32[576,512]{1,0:T(8,128)}, u32[]{:S(2)}) copy-start(f32[576,512]{1,0:T(8,128)} %all-gather.5.cloned.1.call-done) | copy-start | bytes 3538948
  643.1 24.7 %collective-permute-start.4 = (f32[512,512]{1,0:T(8,128)S(1)}, f32[512,512]{1,0:T(8,128)S(1)}, u32[]{:S(2)}, u32[]{:S(2)}) collective-permute-start(f32[512,512]{1,0:T(8,128)S(1)} %fusion.15), channel_id=1, source_target_pairs={{0,8},{8,0},{16,24},{24,16},{32,40},{40,32},{48,56},{56,48},{64,72... | collective-permute-start | bytes 3145736 | tf_op jit(solution)/shard_map/ppermute | solution.py:130
  668.6 25.3 %collective-permute-start.5 = (f32[512,512]{1,0:T(8,128)S(1)}, f32[512,512]{1,0:T(8,128)S(1)}, u32[]{:S(2)}, u32[]{:S(2)}) collective-permute-start(f32[512,512]{1,0:T(8,128)S(1)} %fusion.129), channel_id=1, source_target_pairs={{0,16},{8,24},{16,0},{24,8},{32,48},{40,56},{48,32},{56,40},{64,80... | collective-permute-start | bytes 3145736 | tf_op jit(solution)/shard_map/ppermute | solution.py:130
  694.0 22.9 %collective-permute-start.6 = (f32[512,512]{1,0:T(8,128)S(1)}, f32[512,512]{1,0:T(8,128)S(1)}, u32[]{:S(2)}, u32[]{:S(2)}) collective-permute-start(f32[512,512]{1,0:T(8,128)S(1)} %add.278), channel_id=1, source_target_pairs={{0,32},{8,40},{16,48},{24,56},{32,0},{40,8},{48,16},{56,24},{64,96... | collective-permute-start | bytes 3145736 | tf_op jit(solution)/shard_map/ppermute | solution.py:130
  717.2 24.1 %collective-permute-start.7 = (f32[512,512]{1,0:T(8,128)S(1)}, f32[512,512]{1,0:T(8,128)}, u32[]{:S(2)}, u32[]{:S(2)}) collective-permute-start(f32[512,512]{1,0:T(8,128)S(1)} %add.279), channel_id=1, source_target_pairs={{0,64},{8,72},{16,80},{24,88},{32,96},{40,104},{48,112},{56,120},{... | collective-permute-start | bytes 3145736 | tf_op jit(solution)/shard_map/ppermute | solution.py:130
  749.7 21.7 %copy-start.8 = (f32[512,512]{1,0:T(8,128)S(1)}, f32[512,512]{1,0:T(8,128)}, u32[]{:S(2)}) copy-start(f32[512,512]{1,0:T(8,128)} %copy-done.7) | copy-start | bytes 3145732
  845.4 39.3 %copy-start.6 = (f32[512,512]{1,0:T(8,128)}, f32[512,512]{1,0:T(8,128)S(1)}, u32[]{:S(2)}) copy-start(f32[512,512]{1,0:T(8,128)S(1)} %get-tuple-element.213) | copy-start | bytes 3145732
  890.9 95.7 %copy-start.2 = (f32[576,1152]{1,0:T(8,128)S(1)}, f32[576,1152]{1,0:T(8,128)}, u32[]{:S(2)}) copy-start(f32[576,1152]{1,0:T(8,128)} %copy-done.1) | copy-start | bytes 7962628
  986.6 7.0 copy-start.11
  1006.3 6.5 copy-start.5
  1006.3 24.3 %all-to-all-start.2 = ((f32[8,64,576]{2,1,0:T(8,128)}), f32[8,64,576]{2,1,0:T(8,128)S(1)}, u32[]{:S(2)}, u32[]{:S(2)}) async-start(f32[8,64,576]{2,1,0:T(8,128)} %bitcast.63), calls=%async_computation.4 | async-start | bytes 2621440 | tf_op jit(solution)/shard_map/all_to_all | solution.py:58
  (5 other events, 7.2 us)
Sparse Core Ops, SparseCore 0:
  157.5 26.9 reduce-scatter.2
  186.1 25.4 all-gather.2
  480.0 93.5 all-reduce.7
  584.1 30.2 reduce-scatter.4
  615.9 25.4 all-gather.4
  893.2 93.3 all-reduce.5
